TPU v7x, 256 devices: a whole 4x4x8 slice. The times are simulated.
256 devices in a mesh: gx: 4 (over z_hi, core), gy: 16 (over z_lo, y), gz: 4 (over x).
Axes of the slice: x: 4, y: 4, z: 8 (z_hi: 2, z_lo: 4; z = z_hi * 4 + z_lo), core: 2. Of those that a mesh axis runs over, the one named last changes fastest.
Arguments:
- random_vectors: float32 [64, 128, 128, 128], P('gx', 'gy', 'gz'), may hold values from -6 to 6
- potential: float32 [64, 128, 128], P('gx', 'gy', 'gz'), may hold values from -2.5 to 2.5
Outputs:
- moments: float32 [9, 128], replicated
- chebyshev_vector: float32 [64, 128, 128, 128], P('gx', 'gy', 'gz')
All inputs are finite; a program needn't handle non-finite values.
Results may differ from a plain program's by a relative error of at most 0.0001.
Values sent between devices are 32-bit elements; how exact they have to be, the bound alone decides.
A program may use at most 64 MiB of HBM per device.

v0:
```python
import functools

import jax
import jax.numpy as jnp
from jax import lax
from jax.sharding import Mesh
from jax.sharding import PartitionSpec as P

ITERS = 4
GX_GY_GZ = ("gx_0", "gx_1", "gy_0", "gy_1", "gz")
GX = ("gx_0", "gx_1")
GY = ("gy_0", "gy_1")


def extended(array, sides, width):
    edges = {}
    for axis, dim in sides:
        count, length = (lax.axis_size(axis), array.shape[dim])
        up = [(i, (i + 1) % count) for i in range(count)]
        last = lax.slice_in_dim(array, length - width, length, axis=dim)
        initial = lax.slice_in_dim(array, 0, width, axis=dim)
        edges[dim] = (
            lax.ppermute(last, axis, up),
            lax.ppermute(initial, axis, [(b, a) for a, b in up]),
        )
    done = []
    for _, dim in sides:
        low, high = edges[dim]
        around = [(width, width) if d in done else (0, 0) for d in range(array.ndim)]
        array = jnp.concatenate([jnp.pad(low, around), array, jnp.pad(high, around)], axis=dim)
        done.append(dim)
    return array


def by_axis(array, axes):
    return functools.reduce(lax.psum, axes, array)


def local_product(left, right):
    return jnp.sum(left * right, axis=(0, 1, 2))


def shards(random_vectors, potential):
    onsite = potential[..., None]

    def apply_hamiltonian(field):
        padded = extended(field, ((GX, 0), (GY, 1), ("gz", 2)), 1)
        beside = padded[2:, 1:-1, 1:-1] + padded[:-2, 1:-1, 1:-1]
        beside = beside + padded[1:-1, 2:, 1:-1] + padded[1:-1, :-2, 1:-1]
        beside = beside + padded[1:-1, 1:-1, 2:] + padded[1:-1, 1:-1, :-2]
        return (onsite * field - beside) / 9.0

    sites_total = (
        random_vectors.shape[0]
        * lax.axis_size(GX)
        * (random_vectors.shape[1] * lax.axis_size(GY))
        * (random_vectors.shape[2] * lax.axis_size("gz"))
    )
    highest = ITERS
    terms = [random_vectors]
    while len(terms) <= highest:
        if len(terms) == 1:
            terms.append(apply_hamiltonian(random_vectors))
        else:
            terms.append(2.0 * apply_hamiltonian(terms[-1]) - terms[-2])
    keep = terms[ITERS]
    sums = [local_product(random_vectors, random_vectors), local_product(random_vectors, terms[1])]
    for index in range(1, ITERS):
        sums.append(local_product(terms[index], terms[index]))
        sums.append(local_product(terms[index + 1], terms[index]))
    sums.append(local_product(terms[ITERS], terms[ITERS]))
    totals = by_axis(jnp.stack(sums), GX_GY_GZ)
    order = lax.broadcasted_iota(jnp.int32, totals.shape, 0)
    base = jnp.where(order % 2 == 0, totals[0][None, :], totals[1][None, :])
    moments = jnp.where(order < 2, totals, 2.0 * totals - base) / sites_total
    return (moments, keep)


def solution(mesh):
    split = Mesh(
        mesh.devices.reshape(2, 2, 4, 4, mesh.shape["gz"]), ("gx_0", "gx_1", "gy_0", "gy_1", "gz")
    )
    placed = (P(GX, GY, "gz", None), P(GX, GY, "gz"))
    return jax.shard_map(
        shards, mesh=split, in_specs=placed, out_specs=(P(), P(GX, GY, "gz", None)), check_vma=False
    )
```

profile of v0, /device:TPU:2, one launch (start us, length us, event | category | flops | bytes accessed | tf_op | source)
XLA Modules:
  0.0 146.4 jit_solution(14072577267329621562)
XLA Ops:
  0.6 1.1 fusion.51
  1.9 6.7 %collective-permute-start = (f32[1,8,32,128]{3,2,1,0:T(8,128)S(1)}, f32[1,8,32,128]{3,2,1,0:T(8,128)S(1)}, u32[]{:S(2)}, u32[]{:S(2)}) collective-permute-start(f32[1,8,32,128]{3,2,1,0:T(8,128)S(1)} %get-tuple-element.36), channel_id=1, source_target_pairs={{64,0},{128,64},{192,128},{0,192},{65,1},{129,65},{193,129},{1,193... | collective-permute-start | bytes 393224 | tf_op jit(solution)/shard_map/ppermute | solution.py:24
  8.6 1.1 fusion.50
  9.6 6.1 %collective-permute-start.2 = (f32[16,1,32,128]{3,2,1,0:T(8,128)S(1)}, f32[16,1,32,128]{3,2,1,0:T(8,128)S(1)}, u32[]{:S(2)}, u32[]{:S(2)}) collective-permute-start(f32[16,1,32,128]{3,2,1,0:T(8,128)S(1)} %get-tuple-element.35), channel_id=1, source_target_pairs={{4,0},{8,4},{12,8},{16,12},{20,16},{24,20},{28,24},{32,28},{36,32}... | collective-permute-start | bytes 786440 | tf_op jit(solution)/shard_map/ppermute | solution.py:24
  15.7 1.3 fusion.49
  17.7 1.5 %collective-permute-start.5 = (f32[16,8,1,128]{3,2,1,0:T(1,128)S(1)}, f32[16,8,1,128]{3,2,1,0:T(1,128)S(1)}, u32[]{:S(2)}, u32[]{:S(2)}) collective-permute-start(f32[16,8,1,128]{3,2,1,0:T(1,128)S(1)} %get-tuple-element.33), channel_id=1, source_target_pairs={{0,1},{1,2},{2,3},{3,0},{4,5},{5,6},{6,7},{7,4},{8,9},{9,10},{10,1... | collective-permute-start | bytes 196616 | tf_op jit(solution)/shard_map/ppermute | solution.py:23
  19.4 1.9 %collective-permute-done.2 = f32[16,1,32,128]{3,2,1,0:T(8,128)S(1)} collective-permute-done((f32[16,1,32,128]{3,2,1,0:T(8,128)S(1)}, f32[16,1,32,128]{3,2,1,0:T(8,128)S(1)}, u32[]{:S(2)}, u32[]{:S(2)}) %collective-permute-start.2) | collective-permute-done | bytes 262176 | tf_op jit(solution)/shard_map/ppermute | solution.py:24
  21.4 5.5 %collective-permute-done.3 = f32[16,1,32,128]{3,2,1,0:T(8,128)S(1)} collective-permute-done((f32[16,1,32,128]{3,2,1,0:T(8,128)S(1)}, f32[16,1,32,128]{3,2,1,0:T(8,128)S(1)}, u32[]{:S(2)}, u32[]{:S(2)}) %collective-permute-start.3) | collective-permute-done | bytes 262176 | tf_op jit(solution)/shard_map/ppermute | solution.py:23
  27.0 3.3 %broadcast_multiply_fusion = (f32[16,8,32,128]{3,2,1,0:T(8,128)S(1)}, f32[16,8,32,128]{3,2,1,0:T(8,128)S(1)}) fusion(f32[18,1,32,128]{3,2,1,0:T(8,128)S(1)} %pad.50, f32[18,8,32,128]{3,2,1,0:T(8,128)S(1)} %constant_dynamic-update-slice_fusion, f32[18,1,32,128]{3,2,1,0:T(8,128)S(1)} %pad.51, f32[16,8,1,128]{3,2,1,0:T(1,128)S(1)} %collective-permute-done.5, ...), kind=kLoop, calls=%fused_computation.113 | loop fusion | flops 12582912 | bytes 9650176 | tf_op jit(solution)/shard_map/div | solution.py:51
  30.3 1.7 %collective-permute-start.8 = (f32[16,1,32,128]{3,2,1,0:T(8,128)S(1)}, f32[16,1,32,128]{3,2,1,0:T(8,128)S(1)}, u32[]{:S(2)}, u32[]{:S(2)}) collective-permute-start(f32[16,1,32,128]{3,2,1,0:T(8,128)S(1)} %get-tuple-element.31), channel_id=1, source_target_pairs={{4,0},{8,4},{12,8},{16,12},{20,16},{24,20},{28,24},{32,28},{36,32}... | collective-permute-start | bytes 786440 | tf_op jit(solution)/shard_map/ppermute | solution.py:24
  33.2 2.8 %collective-permute-start.10 = (f32[16,8,1,128]{3,2,1,0:T(1,128)S(1)}, f32[16,8,1,128]{3,2,1,0:T(1,128)S(1)}, u32[]{:S(2)}, u32[]{:S(2)}) collective-permute-start(f32[16,8,1,128]{3,2,1,0:T(1,128)S(1)} %get-tuple-element.26), channel_id=1, source_target_pairs={{1,0},{2,1},{3,2},{0,3},{5,4},{6,5},{7,6},{4,7},{9,8},{10,9},{11,1... | collective-permute-start | bytes 196616 | tf_op jit(solution)/shard_map/ppermute | solution.py:24
  36.0 2.6 %collective-permute-done.8 = f32[16,1,32,128]{3,2,1,0:T(8,128)S(1)} collective-permute-done((f32[16,1,32,128]{3,2,1,0:T(8,128)S(1)}, f32[16,1,32,128]{3,2,1,0:T(8,128)S(1)}, u32[]{:S(2)}, u32[]{:S(2)}) %collective-permute-start.8) | collective-permute-done | bytes 262176 | tf_op jit(solution)/shard_map/ppermute | solution.py:24
  39.1 7.4 %collective-permute-done.9 = f32[16,1,32,128]{3,2,1,0:T(8,128)S(1)} collective-permute-done((f32[16,1,32,128]{3,2,1,0:T(8,128)S(1)}, f32[16,1,32,128]{3,2,1,0:T(8,128)S(1)}, u32[]{:S(2)}, u32[]{:S(2)}) %collective-permute-start.9) | collective-permute-done | bytes 262176 | tf_op jit(solution)/shard_map/ppermute | solution.py:23
  46.6 5.2 %fusion.24 = f32[16,8,32,128]{3,2,1,0:T(8,128)S(1)} fusion(f32[16,8,32,128]{3,2,1,0:T(8,128)S(1)} %copy-done, f32[16,8,1,128]{3,2,1,0:T(1,128)S(1)} %collective-permute-done.11, f32[18,1,32,128]{3,2,1,0:T(8,128)S(1)} %pad.54, f32[18,1,32,128]{3,2,1,0:T(8,128)S(1)} %pad.55, f32[1,8,32,128]{3,2,1,0:T(8,128)S(1)} %collective-permute-done.6, ...), kind=kLoop, calls=%fused_computation.61 | loop fusion | flops 17301504 | bytes 9388032 | tf_op jit(solution)/shard_map/sub | solution.py:65
  51.8 5.5 %collective-permute-start.14 = (f32[16,1,32,128]{3,2,1,0:T(8,128)S(1)}, f32[16,1,32,128]{3,2,1,0:T(8,128)S(1)}, u32[]{:S(2)}, u32[]{:S(2)}) collective-permute-start(f32[16,1,32,128]{3,2,1,0:T(8,128)S(1)} %get-tuple-element.25), channel_id=1, source_target_pairs={{4,0},{8,4},{12,8},{16,12},{20,16},{24,20},{28,24},{32,28},{36,32}... | collective-permute-start | bytes 786440 | tf_op jit(solution)/shard_map/ppermute | solution.py:24
  57.4 1.3 collective-permute-start.12
  58.8 2.7 %collective-permute-start.16 = (f32[16,8,1,128]{3,2,1,0:T(1,128)S(1)}, f32[16,8,1,128]{3,2,1,0:T(1,128)S(1)}, u32[]{:S(2)}, u32[]{:S(2)}) collective-permute-start(f32[16,8,1,128]{3,2,1,0:T(1,128)S(1)} %get-tuple-element.20), channel_id=1, source_target_pairs={{1,0},{2,1},{3,2},{0,3},{5,4},{6,5},{7,6},{4,7},{9,8},{10,9},{11,1... | collective-permute-start | bytes 196616 | tf_op jit(solution)/shard_map/ppermute | solution.py:24
  61.5 3.9 %collective-permute-done.14 = f32[16,1,32,128]{3,2,1,0:T(8,128)S(1)} collective-permute-done((f32[16,1,32,128]{3,2,1,0:T(8,128)S(1)}, f32[16,1,32,128]{3,2,1,0:T(8,128)S(1)}, u32[]{:S(2)}, u32[]{:S(2)}) %collective-permute-start.14) | collective-permute-done | bytes 262176 | tf_op jit(solution)/shard_map/ppermute | solution.py:24
  65.5 5.5 %collective-permute-done.15 = f32[16,1,32,128]{3,2,1,0:T(8,128)S(1)} collective-permute-done((f32[16,1,32,128]{3,2,1,0:T(8,128)S(1)}, f32[16,1,32,128]{3,2,1,0:T(8,128)S(1)}, u32[]{:S(2)}, u32[]{:S(2)}) %collective-permute-start.15) | collective-permute-done | bytes 262176 | tf_op jit(solution)/shard_map/ppermute | solution.py:23
  71.0 5.3 %fusion.14 = f32[16,8,32,128]{3,2,1,0:T(8,128)S(1)} fusion(f32[16,8,1,128]{3,2,1,0:T(1,128)S(1)} %collective-permute-done.17, f32[18,1,32,128]{3,2,1,0:T(8,128)S(1)} %pad.58, f32[18,1,32,128]{3,2,1,0:T(8,128)S(1)} %pad.59, f32[1,8,32,128]{3,2,1,0:T(8,128)S(1)} %collective-permute-done.12, f32[16,8,32,128]{3,2,1,0:T(8,128)S(1)} %fusion.24, ...), kind=kLoop, calls=%fused_computation.33 | loop fusion | flops 17825792 | bytes 7290880 | tf_op jit(solution)/shard_map/sub | solution.py:65
  76.3 6.1 %collective-permute-start.20 = (f32[16,1,32,128]{3,2,1,0:T(8,128)S(1)}, f32[16,1,32,128]{3,2,1,0:T(8,128)S(1)}, u32[]{:S(2)}, u32[]{:S(2)}) collective-permute-start(f32[16,1,32,128]{3,2,1,0:T(8,128)S(1)} %get-tuple-element.17), channel_id=1, source_target_pairs={{4,0},{8,4},{12,8},{16,12},{20,16},{24,20},{28,24},{32,28},{36,32}... | collective-permute-start | bytes 786440 | tf_op jit(solution)/shard_map/ppermute | solution.py:24
  82.6 1.5 %collective-permute-start.18 = (f32[1,8,32,128]{3,2,1,0:T(8,128)S(1)}, f32[1,8,32,128]{3,2,1,0:T(8,128)S(1)}, u32[]{:S(2)}, u32[]{:S(2)}) collective-permute-start(f32[1,8,32,128]{3,2,1,0:T(8,128)S(1)} %get-tuple-element.19), channel_id=1, source_target_pairs={{64,0},{128,64},{192,128},{0,192},{65,1},{129,65},{193,129},{1,193... | collective-permute-start | bytes 393224 | tf_op jit(solution)/shard_map/ppermute | solution.py:24
  84.2 3.1 %collective-permute-start.22 = (f32[16,8,1,128]{3,2,1,0:T(1,128)S(1)}, f32[16,8,1,128]{3,2,1,0:T(1,128)S(1)}, u32[]{:S(2)}, u32[]{:S(2)}) collective-permute-start(f32[16,8,1,128]{3,2,1,0:T(1,128)S(1)} %get-tuple-element.14), channel_id=1, source_target_pairs={{1,0},{2,1},{3,2},{0,3},{5,4},{6,5},{7,6},{4,7},{9,8},{10,9},{11,1... | collective-permute-start | bytes 196616 | tf_op jit(solution)/shard_map/ppermute | solution.py:24
  87.3 3.7 %collective-permute-start.23 = (f32[16,8,1,128]{3,2,1,0:T(1,128)S(1)}, f32[16,8,1,128]{3,2,1,0:T(1,128)S(1)}, u32[]{:S(2)}, u32[]{:S(2)}) collective-permute-start(f32[16,8,1,128]{3,2,1,0:T(1,128)S(1)} %get-tuple-element.15), channel_id=1, source_target_pairs={{0,1},{1,2},{2,3},{3,0},{4,5},{5,6},{6,7},{7,4},{8,9},{9,10},{10,1... | collective-permute-start | bytes 196616 | tf_op jit(solution)/shard_map/ppermute | solution.py:23
  91.1 2.0 %collective-permute-done.21 = f32[16,1,32,128]{3,2,1,0:T(8,128)S(1)} collective-permute-done((f32[16,1,32,128]{3,2,1,0:T(8,128)S(1)}, f32[16,1,32,128]{3,2,1,0:T(8,128)S(1)}, u32[]{:S(2)}, u32[]{:S(2)}) %collective-permute-start.21) | collective-permute-done | bytes 262176 | tf_op jit(solution)/shard_map/ppermute | solution.py:23
  93.7 7.1 %multiply_reduce_fusion = (f32[128]{0:T(128)S(1)}, f32[128]{0:T(128)S(1)}, f32[128]{0:T(128)S(1)}, f32[128]{0:T(128)S(1)}, f32[128]{0:T(128)S(1)}, /*index=5*/f3...) fusion(f32[16,8,32,128]{3,2,1,0:T(8,128)S(1)} %fusion.14, ...), kind=kLoop, calls=%fused_computation.104 | loop fusion | flops 27261824 | bytes 11489792 | tf_op jit(solution)/shard_map/reduce_sum | solution.py:40
  100.8 8.9 %psum.35 = f32[9,128]{1,0:T(8,128)S(1)} all-reduce(f32[9,128]{1,0:T(8,128)S(1)} %stack.39), channel_id=1, replica_groups=mesh['gx_0'=2,'gx_1'=2,'gy_0'=4,'gy_1'=4,'gz'=4] {'gx_0'}, use_global_device_ids=true, to_apply=%region_9.10 | all-reduce | flops 1152 | bytes 9216 | tf_op jit(solution)/shard_map/psum | solution.py:36
  109.7 2.5 %psum.36 = f32[9,128]{1,0:T(8,128)S(1)} all-reduce(f32[9,128]{1,0:T(8,128)S(1)} %psum.35), channel_id=1, replica_groups=mesh['gx_0'=2,'gx_1'=2,'gy_0'=4,'gy_1'=4,'gz'=4] {'gx_1'}, use_global_device_ids=true, to_apply=%region_10.11 | all-reduce | flops 1152 | bytes 9216 | tf_op jit(solution)/shard_map/psum | solution.py:36
  112.2 8.5 %psum.37 = f32[9,128]{1,0:T(8,128)S(1)} all-reduce(f32[9,128]{1,0:T(8,128)S(1)} %psum.36), channel_id=1, replica_groups=mesh['gx_0'=2,'gx_1'=2,'gy_0'=4,'gy_1'=4,'gz'=4] {'gy_0'}, use_global_device_ids=true, to_apply=%region_11.12 | all-reduce | flops 1152 | bytes 9216 | tf_op jit(solution)/shard_map/psum | solution.py:36
  120.7 14.1 %psum.38 = f32[9,128]{1,0:T(8,128)S(1)} all-reduce(f32[9,128]{1,0:T(8,128)S(1)} %psum.37), channel_id=1, replica_groups=mesh['gx_0'=2,'gx_1'=2,'gy_0'=4,'gy_1'=4,'gz'=4] {'gy_1'}, use_global_device_ids=true, to_apply=%region_12.13 | all-reduce | flops 1152 | bytes 9216 | tf_op jit(solution)/shard_map/psum | solution.py:36
  134.8 10.9 %psum.39 = f32[9,128]{1,0:T(8,128)S(1)} all-reduce(f32[9,128]{1,0:T(8,128)S(1)} %psum.38), channel_id=1, replica_groups=mesh['gx_0'=2,'gx_1'=2,'gy_0'=4,'gy_1'=4,'gz'=4] {'gz'}, use_global_device_ids=true, to_apply=%region_13.14 | all-reduce | flops 1152 | bytes 9216 | tf_op jit(solution)/shard_map/psum | solution.py:36
  145.7 0.7 select_multiply_fusion
  (58 shorter events, 4.0 us)
Async XLA Ops:
  0.6 18.5 %copy-start = (f32[16,8,32,128]{3,2,1,0:T(8,128)S(1)}, f32[16,8,32,128]{3,2,1,0:T(8,128)}, u32[]{:S(2)}) copy-start(f32[16,8,32,128]{3,2,1,0:T(8,128)} %param.2) | copy-start | bytes 6291460
  1.8 15.9 %collective-permute-start.1 = (f32[1,8,32,128]{3,2,1,0:T(8,128)S(1)}, f32[1,8,32,128]{3,2,1,0:T(8,128)S(1)}, u32[]{:S(2)}, u32[]{:S(2)}) collective-permute-start(f32[1,8,32,128]{3,2,1,0:T(8,128)S(1)} %get-tuple-element.37), channel_id=1, source_target_pairs={{0,64},{64,128},{128,192},{192,0},{1,65},{65,129},{129,193},{193,1... | collective-permute-start | bytes 393224 | tf_op jit(solution)/shard_map/ppermute | solution.py:23
  1.9 17.6 %collective-permute-start = (f32[1,8,32,128]{3,2,1,0:T(8,128)S(1)}, f32[1,8,32,128]{3,2,1,0:T(8,128)S(1)}, u32[]{:S(2)}, u32[]{:S(2)}) collective-permute-start(f32[1,8,32,128]{3,2,1,0:T(8,128)S(1)} %get-tuple-element.36), channel_id=1, source_target_pairs={{64,0},{128,64},{192,128},{0,192},{65,1},{129,65},{193,129},{1,193... | collective-permute-start | bytes 393224 | tf_op jit(solution)/shard_map/ppermute | solution.py:24
  9.6 11.7 %collective-permute-start.2 = (f32[16,1,32,128]{3,2,1,0:T(8,128)S(1)}, f32[16,1,32,128]{3,2,1,0:T(8,128)S(1)}, u32[]{:S(2)}, u32[]{:S(2)}) collective-permute-start(f32[16,1,32,128]{3,2,1,0:T(8,128)S(1)} %get-tuple-element.35), channel_id=1, source_target_pairs={{4,0},{8,4},{12,8},{16,12},{20,16},{24,20},{28,24},{32,28},{36,32}... | collective-permute-start | bytes 786440 | tf_op jit(solution)/shard_map/ppermute | solution.py:24
  15.7 11.2 %collective-permute-start.3 = (f32[16,1,32,128]{3,2,1,0:T(8,128)S(1)}, f32[16,1,32,128]{3,2,1,0:T(8,128)S(1)}, u32[]{:S(2)}, u32[]{:S(2)}) collective-permute-start(f32[16,1,32,128]{3,2,1,0:T(8,128)S(1)} %get-tuple-element.34), channel_id=1, source_target_pairs={{0,4},{4,8},{8,12},{12,16},{16,20},{20,24},{24,28},{28,32},{32,36}... | collective-permute-start | bytes 786440 | tf_op jit(solution)/shard_map/ppermute | solution.py:23
  17.0 9.9 %collective-permute-start.4 = (f32[16,8,1,128]{3,2,1,0:T(1,128)S(1)}, f32[16,8,1,128]{3,2,1,0:T(1,128)S(1)}, u32[]{:S(2)}, u32[]{:S(2)}) collective-permute-start(f32[16,8,1,128]{3,2,1,0:T(1,128)S(1)} %get-tuple-element.32), channel_id=1, source_target_pairs={{1,0},{2,1},{3,2},{0,3},{5,4},{6,5},{7,6},{4,7},{9,8},{10,9},{11,1... | collective-permute-start | bytes 196616 | tf_op jit(solution)/shard_map/ppermute | solution.py:24
  17.7 9.3 %collective-permute-start.5 = (f32[16,8,1,128]{3,2,1,0:T(1,128)S(1)}, f32[16,8,1,128]{3,2,1,0:T(1,128)S(1)}, u32[]{:S(2)}, u32[]{:S(2)}) collective-permute-start(f32[16,8,1,128]{3,2,1,0:T(1,128)S(1)} %get-tuple-element.33), channel_id=1, source_target_pairs={{0,1},{1,2},{2,3},{3,0},{4,5},{5,6},{6,7},{7,4},{8,9},{9,10},{10,1... | collective-permute-start | bytes 196616 | tf_op jit(solution)/shard_map/ppermute | solution.py:23
  19.2 7.8 %copy-start.1 = (f32[16,8,32]{2,1,0:T(8,128)S(1)}, f32[16,8,32]{2,1,0:T(8,128)}, u32[]{:S(2)}) copy-start(f32[16,8,32]{2,1,0:T(8,128)} %param.3) | copy-start | bytes 49156
  30.3 8.3 %collective-permute-start.8 = (f32[16,1,32,128]{3,2,1,0:T(8,128)S(1)}, f32[16,1,32,128]{3,2,1,0:T(8,128)S(1)}, u32[]{:S(2)}, u32[]{:S(2)}) collective-permute-start(f32[16,1,32,128]{3,2,1,0:T(8,128)S(1)} %get-tuple-element.31), channel_id=1, source_target_pairs={{4,0},{8,4},{12,8},{16,12},{20,16},{24,20},{28,24},{32,28},{36,32}... | collective-permute-start | bytes 786440 | tf_op jit(solution)/shard_map/ppermute | solution.py:24
  32.1 14.4 %collective-permute-start.9 = (f32[16,1,32,128]{3,2,1,0:T(8,128)S(1)}, f32[16,1,32,128]{3,2,1,0:T(8,128)S(1)}, u32[]{:S(2)}, u32[]{:S(2)}) collective-permute-start(f32[16,1,32,128]{3,2,1,0:T(8,128)S(1)} %get-tuple-element.30), channel_id=1, source_target_pairs={{0,4},{4,8},{8,12},{12,16},{16,20},{20,24},{24,28},{28,32},{32,36}... | collective-permute-start | bytes 786440 | tf_op jit(solution)/shard_map/ppermute | solution.py:23
  32.6 13.9 %collective-permute-start.6 = (f32[1,8,32,128]{3,2,1,0:T(8,128)S(1)}, f32[1,8,32,128]{3,2,1,0:T(8,128)S(1)}, u32[]{:S(2)}, u32[]{:S(2)}) collective-permute-start(f32[1,8,32,128]{3,2,1,0:T(8,128)S(1)} %get-tuple-element.29), channel_id=1, source_target_pairs={{64,0},{128,64},{192,128},{0,192},{65,1},{129,65},{193,129},{1,193... | collective-permute-start | bytes 393224 | tf_op jit(solution)/shard_map/ppermute | solution.py:24
  32.7 13.9 %collective-permute-start.7 = (f32[1,8,32,128]{3,2,1,0:T(8,128)S(1)}, f32[1,8,32,128]{3,2,1,0:T(8,128)S(1)}, u32[]{:S(2)}, u32[]{:S(2)}) collective-permute-start(f32[1,8,32,128]{3,2,1,0:T(8,128)S(1)} %get-tuple-element.28), channel_id=1, source_target_pairs={{0,64},{64,128},{128,192},{192,0},{1,65},{65,129},{129,193},{193,1... | collective-permute-start | bytes 393224 | tf_op jit(solution)/shard_map/ppermute | solution.py:23
  33.2 13.3 %collective-permute-start.10 = (f32[16,8,1,128]{3,2,1,0:T(1,128)S(1)}, f32[16,8,1,128]{3,2,1,0:T(1,128)S(1)}, u32[]{:S(2)}, u32[]{:S(2)}) collective-permute-start(f32[16,8,1,128]{3,2,1,0:T(1,128)S(1)} %get-tuple-element.26), channel_id=1, source_target_pairs={{1,0},{2,1},{3,2},{0,3},{5,4},{6,5},{7,6},{4,7},{9,8},{10,9},{11,1... | collective-permute-start | bytes 196616 | tf_op jit(solution)/shard_map/ppermute | solution.py:24
  38.6 7.9 %collective-permute-start.11 = (f32[16,8,1,128]{3,2,1,0:T(1,128)S(1)}, f32[16,8,1,128]{3,2,1,0:T(1,128)S(1)}, u32[]{:S(2)}, u32[]{:S(2)}) collective-permute-start(f32[16,8,1,128]{3,2,1,0:T(1,128)S(1)} %get-tuple-element.27), channel_id=1, source_target_pairs={{0,1},{1,2},{2,3},{3,0},{4,5},{5,6},{6,7},{7,4},{8,9},{9,10},{10,1... | collective-permute-start | bytes 196616 | tf_op jit(solution)/shard_map/ppermute | solution.py:23
  51.8 13.6 %collective-permute-start.14 = (f32[16,1,32,128]{3,2,1,0:T(8,128)S(1)}, f32[16,1,32,128]{3,2,1,0:T(8,128)S(1)}, u32[]{:S(2)}, u32[]{:S(2)}) collective-permute-start(f32[16,1,32,128]{3,2,1,0:T(8,128)S(1)} %get-tuple-element.25), channel_id=1, source_target_pairs={{4,0},{8,4},{12,8},{16,12},{20,16},{24,20},{28,24},{32,28},{36,32}... | collective-permute-start | bytes 786440 | tf_op jit(solution)/shard_map/ppermute | solution.py:24
  57.4 13.6 %collective-permute-start.15 = (f32[16,1,32,128]{3,2,1,0:T(8,128)S(1)}, f32[16,1,32,128]{3,2,1,0:T(8,128)S(1)}, u32[]{:S(2)}, u32[]{:S(2)}) collective-permute-start(f32[16,1,32,128]{3,2,1,0:T(8,128)S(1)} %get-tuple-element.24), channel_id=1, source_target_pairs={{0,4},{4,8},{8,12},{12,16},{16,20},{20,24},{24,28},{28,32},{32,36}... | collective-permute-start | bytes 786440 | tf_op jit(solution)/shard_map/ppermute | solution.py:23
  57.4 13.6 %collective-permute-start.12 = (f32[1,8,32,128]{3,2,1,0:T(8,128)S(1)}, f32[1,8,32,128]{3,2,1,0:T(8,128)S(1)}, u32[]{:S(2)}, u32[]{:S(2)}) collective-permute-start(f32[1,8,32,128]{3,2,1,0:T(8,128)S(1)} %get-tuple-element.23), channel_id=1, source_target_pairs={{64,0},{128,64},{192,128},{0,192},{65,1},{129,65},{193,129},{1,193... | collective-permute-start | bytes 393224 | tf_op jit(solution)/shard_map/ppermute | solution.py:24
  58.7 12.3 %collective-permute-start.13 = (f32[1,8,32,128]{3,2,1,0:T(8,128)S(1)}, f32[1,8,32,128]{3,2,1,0:T(8,128)S(1)}, u32[]{:S(2)}, u32[]{:S(2)}) collective-permute-start(f32[1,8,32,128]{3,2,1,0:T(8,128)S(1)} %get-tuple-element.22), channel_id=1, source_target_pairs={{0,64},{64,128},{128,192},{192,0},{1,65},{65,129},{129,193},{193,1... | collective-permute-start | bytes 393224 | tf_op jit(solution)/shard_map/ppermute | solution.py:23
  58.8 12.1 %collective-permute-start.16 = (f32[16,8,1,128]{3,2,1,0:T(1,128)S(1)}, f32[16,8,1,128]{3,2,1,0:T(1,128)S(1)}, u32[]{:S(2)}, u32[]{:S(2)}) collective-permute-start(f32[16,8,1,128]{3,2,1,0:T(1,128)S(1)} %get-tuple-element.20), channel_id=1, source_target_pairs={{1,0},{2,1},{3,2},{0,3},{5,4},{6,5},{7,6},{4,7},{9,8},{10,9},{11,1... | collective-permute-start | bytes 196616 | tf_op jit(solution)/shard_map/ppermute | solution.py:24
  65.4 5.6 %collective-permute-start.17 = (f32[16,8,1,128]{3,2,1,0:T(1,128)S(1)}, f32[16,8,1,128]{3,2,1,0:T(1,128)S(1)}, u32[]{:S(2)}, u32[]{:S(2)}) collective-permute-start(f32[16,8,1,128]{3,2,1,0:T(1,128)S(1)} %get-tuple-element.21), channel_id=1, source_target_pairs={{0,1},{1,2},{2,3},{3,0},{4,5},{5,6},{6,7},{7,4},{8,9},{9,10},{10,1... | collective-permute-start | bytes 196616 | tf_op jit(solution)/shard_map/ppermute | solution.py:23
  76.3 11.0 %collective-permute-start.20 = (f32[16,1,32,128]{3,2,1,0:T(8,128)S(1)}, f32[16,1,32,128]{3,2,1,0:T(8,128)S(1)}, u32[]{:S(2)}, u32[]{:S(2)}) collective-permute-start(f32[16,1,32,128]{3,2,1,0:T(8,128)S(1)} %get-tuple-element.17), channel_id=1, source_target_pairs={{4,0},{8,4},{12,8},{16,12},{20,16},{24,20},{28,24},{32,28},{36,32}... | collective-permute-start | bytes 786440 | tf_op jit(solution)/shard_map/ppermute | solution.py:24
  82.5 10.6 %collective-permute-start.21 = (f32[16,1,32,128]{3,2,1,0:T(8,128)S(1)}, f32[16,1,32,128]{3,2,1,0:T(8,128)S(1)}, u32[]{:S(2)}, u32[]{:S(2)}) collective-permute-start(f32[16,1,32,128]{3,2,1,0:T(8,128)S(1)} %get-tuple-element.16), channel_id=1, source_target_pairs={{0,4},{4,8},{8,12},{12,16},{16,20},{20,24},{24,28},{28,32},{32,36}... | collective-permute-start | bytes 786440 | tf_op jit(solution)/shard_map/ppermute | solution.py:23
  82.6 10.6 %collective-permute-start.18 = (f32[1,8,32,128]{3,2,1,0:T(8,128)S(1)}, f32[1,8,32,128]{3,2,1,0:T(8,128)S(1)}, u32[]{:S(2)}, u32[]{:S(2)}) collective-permute-start(f32[1,8,32,128]{3,2,1,0:T(8,128)S(1)} %get-tuple-element.19), channel_id=1, source_target_pairs={{64,0},{128,64},{192,128},{0,192},{65,1},{129,65},{193,129},{1,193... | collective-permute-start | bytes 393224 | tf_op jit(solution)/shard_map/ppermute | solution.py:24
  84.1 9.6 %collective-permute-start.19 = (f32[1,8,32,128]{3,2,1,0:T(8,128)S(1)}, f32[1,8,32,128]{3,2,1,0:T(8,128)S(1)}, u32[]{:S(2)}, u32[]{:S(2)}) collective-permute-start(f32[1,8,32,128]{3,2,1,0:T(8,128)S(1)} %get-tuple-element.18), channel_id=1, source_target_pairs={{0,64},{64,128},{128,192},{192,0},{1,65},{65,129},{129,193},{193,1... | collective-permute-start | bytes 393224 | tf_op jit(solution)/shard_map/ppermute | solution.py:23
  84.2 8.9 %collective-permute-start.22 = (f32[16,8,1,128]{3,2,1,0:T(1,128)S(1)}, f32[16,8,1,128]{3,2,1,0:T(1,128)S(1)}, u32[]{:S(2)}, u32[]{:S(2)}) collective-permute-start(f32[16,8,1,128]{3,2,1,0:T(1,128)S(1)} %get-tuple-element.14), channel_id=1, source_target_pairs={{1,0},{2,1},{3,2},{0,3},{5,4},{6,5},{7,6},{4,7},{9,8},{10,9},{11,1... | collective-permute-start | bytes 196616 | tf_op jit(solution)/shard_map/ppermute | solution.py:24
  87.3 5.8 %collective-permute-start.23 = (f32[16,8,1,128]{3,2,1,0:T(1,128)S(1)}, f32[16,8,1,128]{3,2,1,0:T(1,128)S(1)}, u32[]{:S(2)}, u32[]{:S(2)}) collective-permute-start(f32[16,8,1,128]{3,2,1,0:T(1,128)S(1)} %get-tuple-element.15), channel_id=1, source_target_pairs={{0,1},{1,2},{2,3},{3,0},{4,5},{5,6},{6,7},{7,4},{8,9},{9,10},{10,1... | collective-permute-start | bytes 196616 | tf_op jit(solution)/shard_map/ppermute | solution.py:23
where the time goes:
time: 147 us; the launch traced here: 146 us
  starting transfers between devices  45.2 us (31%)
  blocking collectives  44.8 us (30%)
  waiting for transfers between devices  29.4 us (20%)
  other arithmetic  21.5 us (15%)
  local copies, waits for them, and re-layouts  4.41 us (3%)
    psum x5, blocking collectives, by_axis(): return functools.reduce(lax.psum, axes, array)  44.8 us
    ppermute x12, starting transfers between devices, extended(): lax.ppermute(initial, axis, [(b, a) for a, b in up])  38.3 us
    ppermute x12, waiting for transfers between devices, extended(): lax.ppermute(last, axis, up)  21 us
    sub x2, other arithmetic, shards(): terms.append(2.0 * apply_hamiltonian(terms[-1]) - terms[-2])  10.4 us
    ppermute x12, waiting for transfers between devices, extended(): lax.ppermute(initial, axis, [(b, a) for a, b in up])  8.41 us
    reduce_sum x1, other arithmetic, local_product(): return jnp.sum(left * right, axis=(0, 1, 2))  7.09 us
    ppermute x12, starting transfers between devices, extended(): lax.ppermute(last, axis, up)  6.94 us
    div x1, other arithmetic, apply_hamiltonian(): return (onsite * field - beside) / 9.0  3.29 us
  transfers between devices with their start and end apart: 24, of which 9 were waited for; matrix products, arithmetic and copies ran while one was open for 2% of the time, Pallas kernels for 0%

commit v1 on v0

v1 whole, which is shorter than its diff:
```python
import jax
import jax.numpy as jnp
from jax import lax
from jax.experimental import pallas as pl
from jax.experimental.pallas import tpu as pltpu
from jax.sharding import PartitionSpec as P

LX, LY, LZ, R = 16, 8, 32, 128
PX, PY, PZ = LX + 2, LY + 2, 40
ITERS = 4
SITES = 64 * 128 * 128
MESH = pl.DeviceIdType.MESH
XLO, XHI, YLO, YHI, ZLO, ZHI = range(6)


def kernel(v_ref, pot_ref, mom_ref, out_ref, t0, t1, t2, t3, t4, w, zsend, zrecv,
           part, bufa, bufb, load_sem, store_sem, send_sem, recv_sem, asend, arecv, bsend, brecv):
    gx, gy, gz = lax.axis_index("gx"), lax.axis_index("gy"), lax.axis_index("gz")
    t = [t0, t1, t2, t3, t4]
    flat = [r.reshape(PX * PY * PZ, R) for r in t[:4]] + [t4]

    def dev(dx, dy, dz):
        return (lax.rem(gx + dx + 4, 4), lax.rem(gy + dy + 16, 16), lax.rem(gz + dz + 4, 4))

    def inside(ref, x0, x1):
        return ref.at[pl.ds(x0 + 1, x1 - x0), pl.ds(1, LY), pl.ds(0, LZ), :]

    load = pltpu.make_async_copy(v_ref, inside(t0, 0, LX), load_sem)
    load.start()

    row_y = lax.rem(gy, 4)
    row_z = gy // 4
    mine_a = row_y * 4 + gz
    mine_b = row_z * 4 + gx
    peers_a = [(gx, row_z * 4 + lax.rem(row_y + i // 4, 4), lax.rem(gz + i % 4, 4)) for i in range(1, 16)]
    peers_b = [(lax.rem(gx + i % 4, 4), lax.rem(row_z + i // 4, 4) * 4 + row_y, gz) for i in range(1, 16)]
    near = [dev(-1, 0, 0), dev(1, 0, 0), dev(0, -1, 0), dev(0, 1, 0), dev(0, 0, -1), dev(0, 0, 1)]
    barrier = pltpu.get_barrier_semaphore()
    for peer in near + peers_a + peers_b:
        pl.semaphore_signal(barrier, inc=1, device_id=peer, device_id_type=MESH)

    pot_t = jnp.transpose(pot_ref[...].reshape(LX * LY, LZ)) * (2.0 / 9.0)
    for k in range(LX * LY):
        w[k * LZ:(k + 1) * LZ, :] = jnp.broadcast_to(pot_t[:, k:k + 1], (LZ, R))

    pl.semaphore_wait(barrier, 36)
    load.wait()

    def remote(src, dst, n, way, peer):
        return pltpu.make_async_remote_copy(
            src_ref=src, dst_ref=dst, send_sem=send_sem.at[n, way], recv_sem=recv_sem.at[n, way],
            device_id=peer, device_id_type=MESH)

    def xcopies(n):
        r = t[n]
        return [
            remote(r.at[LX, pl.ds(1, LY), pl.ds(0, LZ), :], r.at[0, pl.ds(1, LY), pl.ds(0, LZ), :], n, XLO, near[1]),
            remote(r.at[1, pl.ds(1, LY), pl.ds(0, LZ), :], r.at[LX + 1, pl.ds(1, LY), pl.ds(0, LZ), :], n, XHI, near[0]),
        ]

    def ycopies(n):
        r = t[n]
        return [
            remote(r.at[pl.ds(1, LX), LY, pl.ds(0, LZ), :], r.at[pl.ds(1, LX), 0, pl.ds(0, LZ), :], n, YLO, near[3]),
            remote(r.at[pl.ds(1, LX), 1, pl.ds(0, LZ), :], r.at[pl.ds(1, LX), LY + 1, pl.ds(0, LZ), :], n, YHI, near[2]),
        ]

    def zcopies(n):
        return [
            remote(zsend.at[n, 0], zrecv.at[n, 0], n, ZLO, near[5]),
            remote(zsend.at[n, 1], zrecv.at[n, 1], n, ZHI, near[4]),
        ]

    def zpack(n):
        f = flat[n]
        for x in range(LX):
            base = ((x + 1) * PY + 1) * PZ
            zsend[n, 0, x] = f[pl.ds(base + LZ - 1, LY, stride=PZ), :]
            zsend[n, 1, x] = f[pl.ds(base, LY, stride=PZ), :]

    def zunpack(n):
        f = flat[n]
        for x in range(LX):
            base = ((x + 1) * PY + 1) * PZ
            f[pl.ds(base - 1, LY, stride=PZ), :] = zrecv[n, 0, x]
            f[pl.ds(base + LZ, LY, stride=PZ), :] = zrecv[n, 1, x]

    def columns(n, x, ys, sums):
        cur, nxt = flat[n], flat[n + 1]
        for y in ys:
            base = pl.multiple_of(((x + 1) * PY + y + 1) * PZ, 8)
            wb = pl.multiple_of((x * LY + y) * LZ, 8)
            c = cur[pl.ds(base, LZ), :]
            beside = cur[pl.ds(base - PY * PZ, LZ), :] + cur[pl.ds(base + PY * PZ, LZ), :]
            beside = beside + (cur[pl.ds(base - PZ, LZ), :] + cur[pl.ds(base + PZ, LZ), :])
            beside = beside + (cur[pl.ds(base - 1, LZ), :] + cur[pl.ds(base + 1, LZ), :])
            new = w[pl.ds(wb, LZ), :] * c - (2.0 / 9.0) * beside
            if n == 0:
                new = 0.5 * new
                sums = (sums[0], sums[1], sums[2] + c * c)
            else:
                new = new - flat[n - 1][pl.ds(base, LZ), :]
            nxt[pl.ds(wb if n == ITERS - 1 else base, LZ), :] = new
            sums = (sums[0] + new * c, sums[1] + new * new, sums[2])
        return sums

    copies = []
    for c in xcopies(0) + ycopies(0):
        c.start()
        copies.append(c)
    zpack(0)
    for c in zcopies(0):
        c.start()
        copies.append(c)

    rows = [None] * 9
    for n in range(ITERS):
        for c in zcopies(n) + ycopies(n) + xcopies(n):
            c.wait_recv()
        zunpack(n)
        zero = jnp.zeros((LZ, R), jnp.float32)
        sums = (zero, zero, zero)
        for x in (0, LX - 1):
            sums = columns(n, x, range(LY), sums)
        if n < ITERS - 1:
            for c in xcopies(n + 1):
                c.start()
                copies.append(c)
        sums = lax.fori_loop(1, LX - 1, lambda x, s: columns(n, x, (0, LY - 1), s), sums)
        if n < ITERS - 1:
            for c in ycopies(n + 1):
                c.start()
                copies.append(c)
        sums = lax.fori_loop(1, LX - 1, lambda x, s: columns(n, x, range(1, LY - 1), s), sums)
        if n < ITERS - 1:
            zpack(n + 1)
            for c in zcopies(n + 1):
                c.start()
                copies.append(c)
        if n == 0:
            rows[0] = jnp.sum(sums[2], axis=0, keepdims=True)
        rows[2 * n + 1] = jnp.sum(sums[0], axis=0, keepdims=True)
        rows[2 * n + 2] = jnp.sum(sums[1], axis=0, keepdims=True)

    store = pltpu.make_async_copy(t4.reshape(LX, LY, LZ, R), out_ref, store_sem)
    store.start()

    def gather(peers, buf, mine, ssem, rsem, size):
        outs = []
        for i, peer in enumerate(peers):
            c = pltpu.make_async_remote_copy(
                src_ref=part, dst_ref=buf.at[mine], send_sem=ssem.at[i], recv_sem=rsem.at[mine],
                device_id=peer, device_id_type=MESH)
            c.start()
            outs.append(c)
        return outs

    def arrive(peers_index, buf, mine, rsem, ssem):
        for i in range(1, 16):
            slot = peers_index(i)
            pltpu.make_async_remote_copy(
                src_ref=part, dst_ref=buf.at[slot], send_sem=ssem.at[0], recv_sem=rsem.at[slot],
                device_id=(gx, gy, gz), device_id_type=MESH).wait_recv()

    part[...] = jnp.concatenate(rows + [jnp.zeros((7, R), jnp.float32)], axis=0)
    bufa[mine_a] = part[...]
    outs = gather(peers_a, bufa, mine_a, asend, arecv, 16)
    arrive(lambda i: lax.rem(row_y + i // 4, 4) * 4 + lax.rem(gz + i % 4, 4), bufa, mine_a, arecv, asend)
    for c in outs:
        c.wait_send()
    total = bufa[0]
    for i in range(1, 16):
        total = total + bufa[i]
    part[...] = total
    bufb[mine_b] = total
    outs = gather(peers_b, bufb, mine_b, bsend, brecv, 16)
    arrive(lambda i: lax.rem(row_z + i // 4, 4) * 4 + lax.rem(gx + i % 4, 4), bufb, mine_b, brecv, bsend)
    for c in outs:
        c.wait_send()
    total = bufb[0]
    for i in range(1, 16):
        total = total + bufb[i]
    order = lax.broadcasted_iota(jnp.int32, (16, R), 0)
    base = jnp.where(order % 2 == 0, total[0:1, :], total[1:2, :])
    full = jnp.where(order < 2, total, 2.0 * total - base) * (1.0 / SITES)
    mom_ref[...] = full[:9, :]
    for c in copies:
        c.wait_send()
    store.wait()


def shards(random_vectors, potential):
    padded = pltpu.VMEM((PX, PY, PZ, R), jnp.float32)
    dma = pltpu.SemaphoreType.DMA
    return pl.pallas_call(
        kernel,
        out_shape=(jax.ShapeDtypeStruct((9, R), jnp.float32),
                   jax.ShapeDtypeStruct((LX, LY, LZ, R), jnp.float32)),
        in_specs=[pl.BlockSpec(memory_space=pl.ANY), pl.BlockSpec(memory_space=pltpu.VMEM)],
        out_specs=(pl.BlockSpec(memory_space=pltpu.VMEM), pl.BlockSpec(memory_space=pl.ANY)),
        scratch_shapes=[padded] * 4 + [
            pltpu.VMEM((LX * LY * LZ, R), jnp.float32),
            pltpu.VMEM((LX * LY * LZ, R), jnp.float32),
            pltpu.VMEM((ITERS, 2, LX, LY, R), jnp.float32),
            pltpu.VMEM((ITERS, 2, LX, LY, R), jnp.float32),
            pltpu.VMEM((16, R), jnp.float32),
            pltpu.VMEM((16, 16, R), jnp.float32),
            pltpu.VMEM((16, 16, R), jnp.float32),
            dma, dma, dma((ITERS, 6)), dma((ITERS, 6)),
            dma((16,)), dma((16,)), dma((16,)), dma((16,)),
        ],
        compiler_params=pltpu.CompilerParams(
            collective_id=0, has_side_effects=True, vmem_limit_bytes=48 * 1024 * 1024),
    )(random_vectors, potential)


def solution(mesh):
    placed = (P("gx", "gy", "gz", None), P("gx", "gy", "gz"))
    return jax.shard_map(
        shards, mesh=mesh, in_specs=placed, out_specs=(P(), P("gx", "gy", "gz", None)), check_vma=False)
```

time: 147 us -> 86.3 us (0.59)
  the two profiles are of different devices: /device:TPU:2 before, /device:TPU:1 now
where the time goes in v1:
time: 86.3 us; the launch traced here: 86.1 us
  Pallas kernels  81.1 us (94%)
  local copies, waits for them, and re-layouts  4.34 us (5%)
    pallas_call x1, Pallas kernels, shards(): pl.pallas_call(kernel, out_shape=(jax.ShapeDtypeStruct((9, R), jnp.float3...  81.1 us
    unnamed x6, local copies, waits for them, and re-layouts  4.34 us

profile of v1, /device:TPU:1, one launch (start us, length us, event | category | flops | bytes accessed | tf_op | source)
XLA Modules:
  0.0 86.1 jit_solution(12875505380384045339)
XLA Ops:
  0.6 0.0 copy-start
  0.6 1.6 %copy-done = f32[16,8,32,128]{3,2,1,0:T(8,128)S(1)} copy-done((f32[16,8,32,128]{3,2,1,0:T(8,128)S(1)}, f32[16,8,32,128]{3,2,1,0:T(8,128)}, u32[]{:S(2)}) %copy-start) | copy-done | bytes 2097176
  2.2 0.0 copy-start.1
  2.2 0.8 copy-done.1
  3.1 81.1 %shard_map.41 = (f32[9,128]{1,0:T(8,128)S(1)}, f32[16,8,32,128]{3,2,1,0:T(8,128)S(1)}) custom-call(f32[16,8,32,128]{3,2,1,0:T(8,128)S(1)} %copy-done, f32[16,8,32]{2,1,0:T(8,128)S(1)} %copy-done.1), custom_call_target="tpu_custom_call" | custom-call | tf_op jit(solution)/shard_map/pallas_call | solution.py:195
  84.2 0.6 copy.6
  84.8 1.3 %copy.7 = f32[16,8,32,128]{3,2,1,0:T(8,128)} copy(f32[16,8,32,128]{3,2,1,0:T(8,128)S(1)} %get-tuple-element.5) | data formatting | bytes 4194304
Async XLA Ops:
  0.6 1.6 %copy-start = (f32[16,8,32,128]{3,2,1,0:T(8,128)S(1)}, f32[16,8,32,128]{3,2,1,0:T(8,128)}, u32[]{:S(2)}) copy-start(f32[16,8,32,128]{3,2,1,0:T(8,128)} %v_ref.1) | copy-start | bytes 6291460
  2.2 0.8 copy-start.1

commit v2 on v1

v2 whole, which is shorter than its diff:
```python
import jax
import jax.numpy as jnp
from jax import lax
from jax.experimental import pallas as pl
from jax.experimental.pallas import tpu as pltpu
from jax.sharding import PartitionSpec as P

LX, LY, LZ, R = 16, 8, 32, 128
PX, PY, PZ = LX + 2, LY + 2, 40
HALF = LX // 2
ITERS = 4
SITES = 64 * 128 * 128
MESH = pl.DeviceIdType.MESH
FARA, FARB, NEAR, YLO, YHI, ZLO, ZHI, WAYS = 0, 1, 2, 3, 5, 7, 9, 11


def kernel(v_ref, pot_ref, mom_ref, out_ref, t0, t1, t2, t3, w, pot, zsend, zrecv, relay,
           part, bufa, bufb, load_sem, pot_sem, send_sem, recv_sem, relay_send, relay_recv,
           asend, arecv, bsend, brecv):
    gx, gy, gz = lax.axis_index("gx"), lax.axis_index("gy"), lax.axis_index("gz")
    t = [t0, t1, t2, t3]
    flat = [r.reshape(PX * PY * PZ, R) for r in t] + [out_ref.reshape(LX * LY * LZ, R)]
    par = lax.rem(gx, 2)
    row_y = lax.rem(gy, 4)
    row_z = gy // 4
    far_plane, near_plane = 1 + par * (LX - 1), LX - par * (LX - 1)
    far_halo, near_halo = par * (LX + 1), (1 - par) * (LX + 1)
    x_half = [(1 - par) * HALF, par * HALF]

    def plane(k):
        return k * par + (LX - 1 - k) * (1 - par)

    load = pltpu.make_async_copy(v_ref, t0.at[pl.ds(1, LX), pl.ds(1, LY), pl.ds(0, LZ), :], load_sem)
    load.start()
    load_pot = pltpu.make_async_copy(pot_ref, pot, pot_sem)
    load_pot.start()

    mine_a = row_y * 4 + gz
    mine_b = row_z * 4 + gx
    peers_a = [(gx, row_z * 4 + lax.rem(row_y + i // 4, 4), lax.rem(gz + i % 4, 4)) for i in range(1, 16)]
    peers_b = [(lax.rem(gx + i % 4, 4), lax.rem(row_z + i // 4, 4) * 4 + row_y, gz) for i in range(1, 16)]
    far = (lax.rem(gx + 2 * par + 3, 4), gy, gz)
    near = (gx + 1 - 2 * par, gy, gz)
    ydn, yup = (gx, lax.rem(gy + 15, 16), gz), (gx, lax.rem(gy + 1, 16), gz)
    zdn, zup = (gx, gy, lax.rem(gz + 3, 4)), (gx, gy, lax.rem(gz + 1, 4))
    barrier = pltpu.get_barrier_semaphore()
    side = 1 - 2 * lax.rem(row_y, 2)
    edge = (row_y == 0) | (row_y == 3)
    beside = (gx, gy + side, gz)
    diag = (far[0], gy + side, gz)
    greeted = [far, near, ydn, yup, zdn, zup, diag] + peers_a + peers_b
    for peer in greeted:
        pl.semaphore_signal(barrier, inc=1, device_id=peer, device_id_type=MESH)

    load_pot.wait()
    pot_t = jnp.transpose(pot[...].reshape(LX * LY, LZ)) * (2.0 / 9.0)
    for k in range(LX * LY):
        w[k * LZ:(k + 1) * LZ, :] = jnp.broadcast_to(pot_t[:, k:k + 1], (LZ, R))

    load.wait()
    pl.semaphore_wait(barrier, len(greeted))

    def remote(src, dst, n, way, peer):
        return pltpu.make_async_remote_copy(
            src_ref=src, dst_ref=dst, send_sem=send_sem.at[n, way], recv_sem=recv_sem.at[n, way],
            device_id=peer, device_id_type=MESH)

    def far_copy(n, j):
        ys, zs = pl.ds(1 + j * LY // 2, LY // 2), pl.ds(0, LZ)
        return remote(t[n].at[far_plane, ys, zs, :], t[n].at[(1 - par) * (LX + 1), ys, zs, :], n, FARA + j, far)

    def hop_copy(n):
        return pltpu.make_async_remote_copy(
            src_ref=t[n].at[far_plane, pl.ds(1 + n % 2 * LY // 2, LY // 2), pl.ds(0, LZ), :], dst_ref=relay.at[n],
            send_sem=send_sem.at[n, FARA + n % 2], recv_sem=relay_recv.at[n],
            device_id=beside, device_id_type=MESH)

    def pass_copy(n):
        return pltpu.make_async_remote_copy(
            src_ref=relay.at[n],
            dst_ref=t[n].at[(1 - par) * (LX + 1), pl.ds(1 + n % 2 * LY // 2, LY // 2), pl.ds(0, LZ), :],
            send_sem=relay_send.at[n], recv_sem=recv_sem.at[n, FARA + n % 2],
            device_id=diag, device_id_type=MESH)

    def send_far(n, j):
        if j != n % 2:
            send([far_copy(n, j)])
        else:
            copies.append(far_copy(n, j))
            pl.when(edge)(lambda: hop_copy(n).start())
            pl.when(jnp.logical_not(edge))(lambda: far_copy(n, j).start())

    def forward(n):
        @pl.when(jnp.logical_not(edge))
        def _():
            hop_copy(n).wait_recv()
            pass_copy(n).start()

    def near_copy(n):
        ys, zs = pl.ds(1, LY), pl.ds(0, LZ)
        return remote(t[n].at[near_plane, ys, zs, :], t[n].at[par * (LX + 1), ys, zs, :], n, NEAR, near)

    def y_copies(n, j):
        xs, zs = pl.ds(1 + x_half[j], HALF), pl.ds(0, LZ)
        r = t[n]
        return [remote(r.at[xs, LY, zs, :], r.at[xs, 0, zs, :], n, YLO + j, yup),
                remote(r.at[xs, 1, zs, :], r.at[xs, LY + 1, zs, :], n, YHI + j, ydn)]

    def z_copies(n, j):
        xs = pl.ds(x_half[j], HALF)
        return [remote(zsend.at[n, 0, xs], zrecv.at[n, 0, xs], n, ZLO + j, zup),
                remote(zsend.at[n, 1, xs], zrecv.at[n, 1, xs], n, ZHI + j, zdn)]

    def zpack(n, j):
        f = flat[n]
        for i in range(HALF):
            x = x_half[j] + i
            base = ((x + 1) * PY + 1) * PZ
            zsend[n, 0, x] = f[pl.ds(base + LZ - 1, LY, stride=PZ), :]
            zsend[n, 1, x] = f[pl.ds(base, LY, stride=PZ), :]

    def zunpack(n, j):
        f = flat[n]
        for i in range(HALF):
            x = x_half[j] + i
            base = ((x + 1) * PY + 1) * PZ
            f[pl.ds(base - 1, LY, stride=PZ), :] = zrecv[n, 0, x]
            f[pl.ds(base + LZ, LY, stride=PZ), :] = zrecv[n, 1, x]

    def columns(n, k, ys, sums):
        cur, nxt = flat[n], flat[n + 1]
        x = plane(k)
        for y in ys:
            base = pl.multiple_of(((x + 1) * PY + y + 1) * PZ, 8)
            wb = pl.multiple_of((x * LY + y) * LZ, 8)
            c = cur[pl.ds(base, LZ), :]
            beside = cur[pl.ds(base - PY * PZ, LZ), :] + cur[pl.ds(base + PY * PZ, LZ), :]
            beside = beside + (cur[pl.ds(base - PZ, LZ), :] + cur[pl.ds(base + PZ, LZ), :])
            beside = beside + (cur[pl.ds(base - 1, LZ), :] + cur[pl.ds(base + 1, LZ), :])
            new = w[pl.ds(wb, LZ), :] * c - (2.0 / 9.0) * beside
            if n == 0:
                new = 0.5 * new
                sums = (sums[0], sums[1], sums[2] + c * c)
            else:
                new = new - flat[n - 1][pl.ds(base, LZ), :]
            nxt[pl.ds(wb if n == ITERS - 1 else base, LZ), :] = new
            sums = (sums[0] + new * c, sums[1] + new * new, sums[2])
        return sums

    copies = []

    def send(cs):
        for c in cs:
            c.start()
            copies.append(c)

    def planes(n, lo, hi, ys, sums):
        return lax.fori_loop(lo, hi, lambda k, s: columns(n, k, ys, s), sums)

    send_far(0, 0)
    send_far(0, 1)
    send(y_copies(0, 0) + y_copies(0, 1) + [near_copy(0)])
    for j in range(2):
        zpack(0, j)
        send(z_copies(0, j))
    forward(0)

    def arrived(cs):
        for c in cs:
            c.wait_recv()

    rows = [None] * 9
    outer, inner = (0, LY - 1), range(1, LY - 1)
    for n in range(ITERS):
        more = n < ITERS - 1
        zero = jnp.zeros((LZ, R), jnp.float32)
        sums = (zero, zero, zero)
        arrived(z_copies(n, 0) + [near_copy(n)] + y_copies(n, 0))
        zunpack(n, 0)
        sums = planes(n, 0, HALF, outer, sums)
        if more:
            send(y_copies(n + 1, 0))
        sums = columns(n, 0, inner, sums)
        if more:
            send([near_copy(n + 1)])
        sums = planes(n, 1, HALF, inner, sums)
        if more:
            zpack(n + 1, 0)
            send(z_copies(n + 1, 0))
        arrived(z_copies(n, 1) + y_copies(n, 1))
        zunpack(n, 1)
        for j in range(2):
            arrived([far_copy(n, j)])
            sums = columns(n, LX - 1, range(j * LY // 2, (j + 1) * LY // 2), sums)
            if more:
                send_far(n + 1, j)
        sums = planes(n, HALF, LX - 1, outer, sums)
        if more:
            send(y_copies(n + 1, 1))
        sums = planes(n, HALF, LX - 1, inner, sums)
        if more:
            zpack(n + 1, 1)
            send(z_copies(n + 1, 1))
            forward(n + 1)
        if n == 0:
            rows[0] = jnp.sum(sums[2], axis=0, keepdims=True)
        rows[2 * n + 1] = jnp.sum(sums[0], axis=0, keepdims=True)
        rows[2 * n + 2] = jnp.sum(sums[1], axis=0, keepdims=True)

    def gather(peers, buf, mine, ssem, rsem):
        outs = []
        for i, peer in enumerate(peers):
            c = pltpu.make_async_remote_copy(
                src_ref=part, dst_ref=buf.at[mine], send_sem=ssem.at[i], recv_sem=rsem.at[mine],
                device_id=peer, device_id_type=MESH)
            c.start()
            outs.append(c)
        return outs

    def arrive(slots, peers, buf, rsem, ssem):
        for slot, peer in zip(slots, peers):
            pltpu.make_async_remote_copy(
                src_ref=part, dst_ref=buf.at[slot], send_sem=ssem.at[0], recv_sem=rsem.at[slot],
                device_id=peer, device_id_type=MESH).wait_recv()

    part[...] = jnp.concatenate(rows, axis=0)
    bufa[mine_a] = part[...]
    outs = gather(peers_a, bufa, mine_a, asend, arecv)
    arrive([lax.rem(row_y + i // 4, 4) * 4 + lax.rem(gz + i % 4, 4) for i in range(1, 16)], peers_a, bufa, arecv, asend)
    for c in outs:
        c.wait_send()
    total = bufa[0]
    for i in range(1, 16):
        total = total + bufa[i]
    part[...] = total
    bufb[mine_b] = total
    outs = gather(peers_b, bufb, mine_b, bsend, brecv)
    arrive([lax.rem(row_z + i // 4, 4) * 4 + lax.rem(gx + i % 4, 4) for i in range(1, 16)], peers_b, bufb, brecv, bsend)
    for c in outs:
        c.wait_send()
    total = bufb[0]
    for i in range(1, 16):
        total = total + bufb[i]
    order = lax.broadcasted_iota(jnp.int32, (9, R), 0)
    base = jnp.where(order % 2 == 0, total[0:1, :], total[1:2, :])
    mom_ref[...] = jnp.where(order < 2, total, 2.0 * total - base) * (1.0 / SITES)
    for c in copies:
        c.wait_send()

    @pl.when(jnp.logical_not(edge))
    def _():
        for n in range(ITERS):
            pass_copy(n).wait_send()


def shards(random_vectors, potential):
    padded = pltpu.VMEM((PX, PY, PZ, R), jnp.float32)
    dma = pltpu.SemaphoreType.DMA
    return pl.pallas_call(
        kernel,
        out_shape=(jax.ShapeDtypeStruct((9, R), jnp.float32),
                   jax.ShapeDtypeStruct((LX, LY, LZ, R), jnp.float32)),
        in_specs=[pl.BlockSpec(memory_space=pltpu.MemorySpace.HBM)] * 2,
        out_specs=(pl.BlockSpec(memory_space=pltpu.VMEM), pl.BlockSpec(memory_space=pltpu.VMEM)),
        scratch_shapes=[padded] * 4 + [
            pltpu.VMEM((LX * LY * LZ, R), jnp.float32),
            pltpu.VMEM((LX, LY, LZ), jnp.float32),
            pltpu.VMEM((ITERS, 2, LX, LY, R), jnp.float32),
            pltpu.VMEM((ITERS, 2, LX, LY, R), jnp.float32),
            pltpu.VMEM((ITERS, LY // 2, LZ, R), jnp.float32),
            pltpu.VMEM((9, R), jnp.float32),
            pltpu.VMEM((16, 9, R), jnp.float32),
            pltpu.VMEM((16, 9, R), jnp.float32),
            dma, dma, dma((ITERS, WAYS)), dma((ITERS, WAYS)), dma((ITERS,)), dma((ITERS,)),
            dma((16,)), dma((16,)), dma((16,)), dma((16,)),
        ],
        compiler_params=pltpu.CompilerParams(
            collective_id=0, has_side_effects=True, vmem_limit_bytes=48 * 1024 * 1024),
    )(random_vectors, potential)


def solution(mesh):
    placed = (P("gx", "gy", "gz", None), P("gx", "gy", "gz"))
    return jax.shard_map(
        shards, mesh=mesh, in_specs=placed, out_specs=(P(), P("gx", "gy", "gz", None)), check_vma=False)
```

time: 86.3 us -> 72.8 us (0.84)
  Pallas kernels: 81.1 us -> 67.7 us
    pallas_call x1, Pallas kernels: 81.1 us -> 67.7 us  [shards(): pl.pallas_call(kernel, out_shape=(jax.ShapeDtypeStruct((9, R), jnp.float3...]
where the time goes in v2:
time: 72.8 us; the launch traced here: 72.7 us
  Pallas kernels  67.7 us (93%)
  local copies, waits for them, and re-layouts  4.34 us (6%)
    pallas_call x1, Pallas kernels, shards(): pl.pallas_call(kernel, out_shape=(jax.ShapeDtypeStruct((9, R), jnp.float3...  67.7 us
    unnamed x6, local copies, waits for them, and re-layouts  4.34 us

profile of v2, /device:TPU:1, one launch (start us, length us, event | category | flops | bytes accessed | tf_op | source)
XLA Modules:
  0.0 72.7 jit_solution(5371805663418425693)
XLA Ops:
  0.6 0.0 copy-start
  0.6 1.6 %copy-done = f32[16,8,32,128]{3,2,1,0:T(8,128)S(1)} copy-done((f32[16,8,32,128]{3,2,1,0:T(8,128)S(1)}, f32[16,8,32,128]{3,2,1,0:T(8,128)}, u32[]{:S(2)}) %copy-start) | copy-done | bytes 2097176
  2.2 0.0 copy-start.1
  2.2 0.8 %copy-done.1 = f32[16,8,32]{2,1,0:T(8,128)S(1)} copy-done((f32[16,8,32]{2,1,0:T(8,128)S(1)}, f32[16,8,32]{2,1,0:T(8,128)}, u32[]{:S(2)}) %copy-start.1) | copy-done | bytes 16408
  3.1 67.7 %shard_map.41 = (f32[9,128]{1,0:T(8,128)S(1)}, f32[16,8,32,128]{3,2,1,0:T(8,128)S(1)}) custom-call(f32[16,8,32,128]{3,2,1,0:T(8,128)S(1)} %copy-done, f32[16,8,32]{2,1,0:T(8,128)S(1)} %copy-done.1), custom_call_target="tpu_custom_call" | custom-call | tf_op jit(solution)/shard_map/pallas_call | solution.py:259
  70.7 0.6 copy.6
  71.3 1.3 %copy.7 = f32[16,8,32,128]{3,2,1,0:T(8,128)} copy(f32[16,8,32,128]{3,2,1,0:T(8,128)S(1)} %get-tuple-element.5) | data formatting | bytes 4194304
Async XLA Ops:
  0.6 1.6 %copy-start = (f32[16,8,32,128]{3,2,1,0:T(8,128)S(1)}, f32[16,8,32,128]{3,2,1,0:T(8,128)}, u32[]{:S(2)}) copy-start(f32[16,8,32,128]{3,2,1,0:T(8,128)} %v_ref.1) | copy-start | bytes 6291460
  2.2 0.8 %copy-start.1 = (f32[16,8,32]{2,1,0:T(8,128)S(1)}, f32[16,8,32]{2,1,0:T(8,128)}, u32[]{:S(2)}) copy-start(f32[16,8,32]{2,1,0:T(8,128)} %pot_ref.1) | copy-start | bytes 49156

commit v3 on v2

v3 whole, which is shorter than its diff:
```python
import jax
import jax.numpy as jnp
from jax import lax
from jax.experimental import pallas as pl
from jax.experimental.pallas import tpu as pltpu
from jax.sharding import PartitionSpec as P

LX, LY, LZ, R = 16, 8, 32, 128
ITERS = 4
PX, PY, PZ = LX + 1 + ITERS, LY + 2, 40
CUTS = (0, LX // 2, LX - 1)
SITES = 64 * 128 * 128
MESH = pl.DeviceIdType.MESH
COPIES = 88
LIMIT = 48 * 1024 * 1024


def kernel(v_ref, pot_ref, mom_ref, out_ref, t0, t1, t2, t3, w, pot, pot_halo, zsend, zrecv, dsend, drecv, relay,
           part, bufa, bufb, load_sem, pot_sem, send_sem, recv_sem, asend, arecv, bsend, brecv):
    gx, gy, gz = lax.axis_index("gx"), lax.axis_index("gy"), lax.axis_index("gz")
    t = [t0, t1, t2, t3]
    flat = [r.reshape(PX * PY * PZ, R) for r in t] + [out_ref.reshape(LX * LY * LZ, R)]
    par = lax.rem(gx, 2)
    row_y = lax.rem(gy, 4)
    row_z = gy // 4

    def plane(k):
        return k * par + (LX - 1 - k) * (1 - par)

    loads = [pltpu.make_async_copy(v_ref.at[plane(k)], t0.at[k + 1, pl.ds(1, LY), pl.ds(0, LZ), :], load_sem.at[k])
             for k in range(LX)]
    for c in loads:
        c.start()
    load_pot = pltpu.make_async_copy(pot_ref, pot, pot_sem)
    load_pot.start()

    mine_a = row_y * 4 + gz
    mine_b = row_z * 4 + gx
    peers_a = [(gx, row_z * 4 + lax.rem(row_y + i // 4, 4), lax.rem(gz + i % 4, 4)) for i in range(1, 16)]
    peers_b = [(lax.rem(gx + i % 4, 4), lax.rem(row_z + i // 4, 4) * 4 + row_y, gz) for i in range(1, 16)]
    far = (lax.rem(gx + 2 * par + 3, 4), gy, gz)
    near = (gx + 1 - 2 * par, gy, gz)
    ydn, yup = (gx, lax.rem(gy + 15, 16), gz), (gx, lax.rem(gy + 1, 16), gz)
    zdn, zup = (gx, gy, lax.rem(gz + 3, 4)), (gx, gy, lax.rem(gz + 1, 4))
    barrier = pltpu.get_barrier_semaphore()
    side = 1 - 2 * lax.rem(row_y, 2)
    edge = (row_y == 0) | (row_y == 3)
    beside = (gx, gy + side, gz)
    diag = (far[0], gy + side, gz)
    greeted = [far, near, ydn, yup, zdn, zup, diag] + peers_a + peers_b
    for peer in greeted:
        pl.semaphore_signal(barrier, inc=1, device_id=peer, device_id_type=MESH)

    load_pot.wait()
    for c in loads:
        c.wait()
    pl.semaphore_wait(barrier, len(greeted))

    index = {}

    def remote(key, src, dst, peer):
        i = index.setdefault(key, len(index))
        return pltpu.make_async_remote_copy(
            src_ref=src, dst_ref=dst, send_sem=send_sem.at[i], recv_sem=recv_sem.at[i],
            device_id=peer, device_id_type=MESH)

    rows_z = pl.ds(0, LZ)
    halves = [pl.ds(1, LY // 2), pl.ds(1 + LY // 2, LY // 2)]

    def far_copy(p, j):
        return remote(("far", p, j), t0.at[LX - p, halves[j], rows_z, :], t0.at[LX + 1 + p, halves[j], rows_z, :], far)

    def hop_copy(p):
        return remote(("hop", p), t0.at[LX - p, halves[1], rows_z, :], relay.at[p], beside)

    def pass_copy(p):
        i, k = index.setdefault(("pass", p), len(index)), index[("far", p, 1)]
        return pltpu.make_async_remote_copy(
            src_ref=relay.at[p], dst_ref=t0.at[LX + 1 + p, halves[1], rows_z, :],
            send_sem=send_sem.at[i], recv_sem=recv_sem.at[k], device_id=diag, device_id_type=MESH)

    def near_copy(n):
        return remote(("near", n), t[n].at[1, pl.ds(1, LY), rows_z, :], t[n].at[0, pl.ds(1, LY), rows_z, :], near)

    def y_pair(name, n, ks):
        r = t[n]
        return [remote(name + ("lo",), r.at[ks, LY, rows_z, :], r.at[ks, 0, rows_z, :], yup),
                remote(name + ("hi",), r.at[ks, 1, rows_z, :], r.at[ks, LY + 1, rows_z, :], ydn)]

    def y_copies(n, j):
        return y_pair(("y", n, j), n, pl.ds(1 + CUTS[j], CUTS[j + 1] - CUTS[j]))

    def z_copies(n, j):
        ks = pl.ds(CUTS[j], CUTS[j + 1] - CUTS[j])
        return [remote(("z", n, j, "lo"), zsend.at[n, 0, ks], zrecv.at[n, 0, ks], zup),
                remote(("z", n, j, "hi"), zsend.at[n, 1, ks], zrecv.at[n, 1, ks], zdn)]

    def skew(p):
        return [(m, LX - 1 + p - m) for m in range(p + 1)]

    def skew_y(p):
        return [c for m, k in skew(p) for c in y_pair(("dy", p, m), m, k + 1)]

    def skew_z(p):
        ms = pl.ds(0, p + 1)
        return [remote(("dz", p, "lo"), dsend.at[p, 0, ms], drecv.at[p, 0, ms], zup),
                remote(("dz", p, "hi"), dsend.at[p, 1, ms], drecv.at[p, 1, ms], zdn)]

    def pot_copy(i):
        return remote(("pot", i), pot.at[plane(LX - 1 - i)], pot_halo.at[i], far)

    def ends(n, k):
        base = ((k + 1) * PY + 1) * PZ
        return flat[n][pl.ds(base + LZ - 1, LY, stride=PZ), :], flat[n][pl.ds(base, LY, stride=PZ), :]

    def set_ends(n, k, lo, hi):
        base = ((k + 1) * PY + 1) * PZ
        flat[n][pl.ds(base - 1, LY, stride=PZ), :] = lo
        flat[n][pl.ds(base + LZ, LY, stride=PZ), :] = hi

    def zpack(n, j):
        for k in range(CUTS[j], CUTS[j + 1]):
            zsend[n, 0, k], zsend[n, 1, k] = ends(n, k)

    def zunpack(n, j):
        for k in range(CUTS[j], CUTS[j + 1]):
            set_ends(n, k, zrecv[n, 0, k], zrecv[n, 1, k])

    def skew_pack(p):
        for m, k in skew(p):
            dsend[p, 0, m], dsend[p, 1, m] = ends(m, k)

    def skew_unpack(p):
        for m, k in skew(p):
            set_ends(m, k, drecv[p, 0, m], drecv[p, 1, m])

    def columns(n, k, ys, sums):
        cur, nxt = flat[n], flat[n + 1]
        for y in ys:
            base = pl.multiple_of(((k + 1) * PY + y + 1) * PZ, 8)
            c = cur[pl.ds(base, LZ), :]
            beside = cur[pl.ds(base - PY * PZ, LZ), :] + cur[pl.ds(base + PY * PZ, LZ), :]
            beside = beside + (cur[pl.ds(base - PZ, LZ), :] + cur[pl.ds(base + PZ, LZ), :])
            beside = beside + (cur[pl.ds(base - 1, LZ), :] + cur[pl.ds(base + 1, LZ), :])
            new = w[pl.ds(pl.multiple_of((k * LY + y) * LZ, 8), LZ), :] * c - (2.0 / 9.0) * beside
            if n == 0:
                new = 0.5 * new
            else:
                new = new - flat[n - 1][pl.ds(base, LZ), :]
            if n == ITERS - 1:
                nxt[pl.ds(pl.multiple_of((plane(k) * LY + y) * LZ, 8), LZ), :] = new
            else:
                nxt[pl.ds(base, LZ), :] = new
            if sums is not None:
                sums = (sums[0] + new * c, sums[1] + new * new, sums[2] + c * c if n == 0 else sums[2])
        return sums

    copies = []

    def send(cs):
        for c in cs:
            c.start()
            copies.append(c)

    def planes(n, lo, hi, ys, sums):
        return lax.fori_loop(lo, hi, lambda k, s: columns(n, k, ys, s), sums)

    def send_far(p):
        send([far_copy(p, 0)])
        direct = far_copy(p, 1)
        hop = hop_copy(p)

        @pl.when(edge)
        def _():
            hop.start()

        @pl.when(jnp.logical_not(edge))
        def _():
            direct.start()

    def forward(p):
        @pl.when(jnp.logical_not(edge))
        def _():
            hop_copy(p).wait_recv()
            pass_copy(p).start()

    def arrived(cs):
        for c in cs:
            c.wait_recv()

    send_far(0)
    for j in range(2):
        send(y_copies(0, j))
    send(skew_y(0) + [near_copy(0)])
    for j in range(2):
        zpack(0, j)
        send(z_copies(0, j))
    skew_pack(0)
    send(skew_z(0) + [pot_copy(i) for i in range(ITERS - 1)])
    send_far(1)

    pot_t = jnp.transpose(pot[...].reshape(LX * LY, LZ)) * (2.0 / 9.0)
    for x in range(LX):
        for y in range(LY):
            start = pl.multiple_of((plane(x) * LY + y) * LZ, 8)
            w[pl.ds(start, LZ), :] = jnp.broadcast_to(pot_t[:, x * LY + y:x * LY + y + 1], (LZ, R))
    forward(0)

    rows = [None] * 9
    outer, inner = (0, LY - 1), range(1, LY - 1)
    for n in range(ITERS):
        more = n < ITERS - 1
        zero = jnp.zeros((LZ, R), jnp.float32)
        sums = (zero, zero, zero)
        arrived(z_copies(n, 0) + [near_copy(n)] + y_copies(n, 0))
        zunpack(n, 0)
        sums = planes(n, CUTS[0], CUTS[1], outer, sums)
        if more:
            send(y_copies(n + 1, 0))
        arrived(z_copies(n, 1) + y_copies(n, 1))
        zunpack(n, 1)
        sums = planes(n, CUTS[1], CUTS[2], outer, sums)
        if more:
            send(y_copies(n + 1, 1))
        if n + 2 < ITERS:
            send_far(n + 2)
        if more:
            forward(n + 1)
        sums = columns(n, 0, inner, sums)
        if more:
            send([near_copy(n + 1)])
        sums = planes(n, 1, CUTS[1], inner, sums)
        if more:
            zpack(n + 1, 0)
            send(z_copies(n + 1, 0))
        sums = planes(n, CUTS[1], CUTS[2], inner, sums)
        if more:
            zpack(n + 1, 1)
            send(z_copies(n + 1, 1))
        if n == 1:
            arrived([pot_copy(i) for i in range(ITERS - 1)])
            halo_t = jnp.transpose(pot_halo[...].reshape((ITERS - 1) * LY, LZ)) * (2.0 / 9.0)
            for i in range((ITERS - 1) * LY):
                start = (LX * LY + i) * LZ
                w[start:start + LZ, :] = jnp.broadcast_to(halo_t[:, i:i + 1], (LZ, R))
        arrived(skew_z(n) + skew_y(n))
        skew_unpack(n)
        arrived([far_copy(n, 0), far_copy(n, 1)])
        for m, k in skew(n):
            if m < n:
                columns(m, k, range(LY), None)
            else:
                sums = columns(m, k, range(LY), sums)
        if more:
            send(skew_y(n + 1))
            skew_pack(n + 1)
            send(skew_z(n + 1))
        if n == 0:
            rows[0] = jnp.sum(sums[2], axis=0, keepdims=True)
        rows[2 * n + 1] = jnp.sum(sums[0], axis=0, keepdims=True)
        rows[2 * n + 2] = jnp.sum(sums[1], axis=0, keepdims=True)

    def gather(peers, buf, mine, ssem, rsem):
        outs = []
        for i, peer in enumerate(peers):
            c = pltpu.make_async_remote_copy(
                src_ref=part, dst_ref=buf.at[mine], send_sem=ssem.at[i], recv_sem=rsem.at[mine],
                device_id=peer, device_id_type=MESH)
            c.start()
            outs.append(c)
        return outs

    def arrive(slots, peers, buf, rsem, ssem):
        for slot, peer in zip(slots, peers):
            pltpu.make_async_remote_copy(
                src_ref=part, dst_ref=buf.at[slot], send_sem=ssem.at[0], recv_sem=rsem.at[slot],
                device_id=peer, device_id_type=MESH).wait_recv()

    part[...] = jnp.concatenate(rows, axis=0)
    bufa[mine_a] = part[...]
    outs = gather(peers_a, bufa, mine_a, asend, arecv)
    arrive([lax.rem(row_y + i // 4, 4) * 4 + lax.rem(gz + i % 4, 4) for i in range(1, 16)], peers_a, bufa, arecv, asend)
    for c in outs:
        c.wait_send()
    total = bufa[0]
    for i in range(1, 16):
        total = total + bufa[i]
    part[...] = total
    bufb[mine_b] = total
    outs = gather(peers_b, bufb, mine_b, bsend, brecv)
    arrive([lax.rem(row_z + i // 4, 4) * 4 + lax.rem(gx + i % 4, 4) for i in range(1, 16)], peers_b, bufb, brecv, bsend)
    for c in outs:
        c.wait_send()
    total = bufb[0]
    for i in range(1, 16):
        total = total + bufb[i]
    order = lax.broadcasted_iota(jnp.int32, (9, R), 0)
    base = jnp.where(order % 2 == 0, total[0:1, :], total[1:2, :])
    mom_ref[...] = jnp.where(order < 2, total, 2.0 * total - base) * (1.0 / SITES)
    for c in copies:
        c.wait_send()

    @pl.when(edge)
    def _():
        for p in range(ITERS):
            hop_copy(p).wait_send()

    @pl.when(jnp.logical_not(edge))
    def _():
        for p in range(ITERS):
            far_copy(p, 1).wait_send()
            pass_copy(p).wait_send()


def shards(random_vectors, potential):
    padded = pltpu.VMEM((PX, PY, PZ, R), jnp.float32)
    dma = pltpu.SemaphoreType.DMA
    return pl.pallas_call(
        kernel,
        out_shape=(jax.ShapeDtypeStruct((9, R), jnp.float32),
                   jax.ShapeDtypeStruct((LX, LY, LZ, R), jnp.float32)),
        in_specs=[pl.BlockSpec(memory_space=pltpu.MemorySpace.HBM)] * 2,
        out_specs=(pl.BlockSpec(memory_space=pltpu.VMEM), pl.BlockSpec(memory_space=pltpu.VMEM)),
        scratch_shapes=[padded] * 4 + [
            pltpu.VMEM(((LX + ITERS - 1) * LY * LZ, R), jnp.float32),
            pltpu.VMEM((LX, LY, LZ), jnp.float32),
            pltpu.VMEM((ITERS - 1, LY, LZ), jnp.float32),
            pltpu.VMEM((ITERS, 2, LX, LY, R), jnp.float32),
            pltpu.VMEM((ITERS, 2, LX, LY, R), jnp.float32),
            pltpu.VMEM((ITERS, 2, ITERS, LY, R), jnp.float32),
            pltpu.VMEM((ITERS, 2, ITERS, LY, R), jnp.float32),
            pltpu.VMEM((ITERS, LY // 2, LZ, R), jnp.float32),
            pltpu.VMEM((9, R), jnp.float32),
            pltpu.VMEM((16, 9, R), jnp.float32),
            pltpu.VMEM((16, 9, R), jnp.float32),
            dma((LX,)), dma, dma((COPIES,)), dma((COPIES,)),
            dma((16,)), dma((16,)), dma((16,)), dma((16,)),
        ],
        compiler_params=pltpu.CompilerParams(
            collective_id=0, has_side_effects=True, vmem_limit_bytes=LIMIT),
    )(pltpu.with_memory_space_constraint(random_vectors, pltpu.HBM), pltpu.with_memory_space_constraint(potential, pltpu.HBM))


def solution(mesh):
    placed = (P("gx", "gy", "gz", None), P("gx", "gy", "gz"))
    return jax.shard_map(
        shards, mesh=mesh, in_specs=placed, out_specs=(P(), P("gx", "gy", "gz", None)), check_vma=False)
```

time: 72.8 us -> 70.1 us (0.963)
  local copies, waits for them, and re-layouts: 4.34 us -> 1.92 us
    unnamed x6 -> x2, local copies, waits for them, and re-layouts: 4.34 us -> 1.92 us
where the time goes in v3:
time: 70.1 us; the launch traced here: 70 us
  Pallas kernels  67.5 us (96%)
  local copies, waits for them, and re-layouts  1.92 us (3%)
    pallas_call x1, Pallas kernels, shards(): pl.pallas_call(kernel, out_shape=(jax.ShapeDtypeStruct((9, R), jnp.float3...  67.5 us
    unnamed x2, local copies, waits for them, and re-layouts  1.92 us

profile of v3, /device:TPU:1, one launch (start us, length us, event | category | flops | bytes accessed | tf_op | source)
XLA Modules:
  0.0 70.0 jit_solution(4683904096832494914)
XLA Ops:
  0.6 67.5 %shard_map.41 = (f32[9,128]{1,0:T(8,128)S(1)}, f32[16,8,32,128]{3,2,1,0:T(8,128)S(1)}) custom-call(f32[16,8,32,128]{3,2,1,0:T(8,128)} %v_ref.1, f32[16,8,32]{2,1,0:T(8,128)} %pot_ref.1), custom_call_target="tpu_custom_call" | custom-call | tf_op jit(solution)/shard_map/pallas_call | solution.py:318
  68.1 0.6 copy.6
  68.7 1.3 %copy.7 = f32[16,8,32,128]{3,2,1,0:T(8,128)} copy(f32[16,8,32,128]{3,2,1,0:T(8,128)S(1)} %get-tuple-element.5) | data formatting | bytes 4194304

commit v4 on v3

--- a/solution.py
+++ b/solution.py
@@ -197,7 +197,6 @@
         send(z_copies(0, j))
     skew_pack(0)
     send(skew_z(0) + [pot_copy(i) for i in range(ITERS - 1)])
-    send_far(1)
 
     pot_t = jnp.transpose(pot[...].reshape(LX * LY, LZ)) * (2.0 / 9.0)
     for x in range(LX):
@@ -217,15 +216,12 @@
         sums = planes(n, CUTS[0], CUTS[1], outer, sums)
         if more:
             send(y_copies(n + 1, 0))
+            send_far(n + 1)
         arrived(z_copies(n, 1) + y_copies(n, 1))
         zunpack(n, 1)
         sums = planes(n, CUTS[1], CUTS[2], outer, sums)
         if more:
             send(y_copies(n + 1, 1))
-        if n + 2 < ITERS:
-            send_far(n + 2)
-        if more:
-            forward(n + 1)
         sums = columns(n, 0, inner, sums)
         if more:
             send([near_copy(n + 1)])
@@ -243,6 +239,8 @@
             for i in range((ITERS - 1) * LY):
                 start = (LX * LY + i) * LZ
                 w[start:start + LZ, :] = jnp.broadcast_to(halo_t[:, i:i + 1], (LZ, R))
+        if more:
+            forward(n + 1)
         arrived(skew_z(n) + skew_y(n))
         skew_unpack(n)
         arrived([far_copy(n, 0), far_copy(n, 1)])

time: 70.1 us -> 67 us (0.956)
  Pallas kernels: 67.5 us -> 64.3 us
    pallas_call x1, Pallas kernels: 67.5 us -> 64.3 us  [shards(): pl.pallas_call(kernel, out_shape=(jax.ShapeDtypeStruct((9, R), jnp.float3...]
where the time goes in v4:
time: 67 us; the launch traced here: 66.9 us
  Pallas kernels  64.3 us (96%)
  local copies, waits for them, and re-layouts  1.92 us (3%)
    pallas_call x1, Pallas kernels, shards(): pl.pallas_call(kernel, out_shape=(jax.ShapeDtypeStruct((9, R), jnp.float3...  64.3 us
    unnamed x2, local copies, waits for them, and re-layouts  1.92 us

profile of v4, /device:TPU:1, one launch (start us, length us, event | category | flops | bytes accessed | tf_op | source)
XLA Modules:
  0.0 66.9 jit_solution(1864864664462962290)
XLA Ops:
  0.6 64.3 %shard_map.41 = (f32[9,128]{1,0:T(8,128)S(1)}, f32[16,8,32,128]{3,2,1,0:T(8,128)S(1)}) custom-call(f32[16,8,32,128]{3,2,1,0:T(8,128)} %v_ref.1, f32[16,8,32]{2,1,0:T(8,128)} %pot_ref.1), custom_call_target="tpu_custom_call" | custom-call | tf_op jit(solution)/shard_map/pallas_call | solution.py:316
  65.0 0.6 copy.6
  65.6 1.3 %copy.7 = f32[16,8,32,128]{3,2,1,0:T(8,128)} copy(f32[16,8,32,128]{3,2,1,0:T(8,128)S(1)} %get-tuple-element.5) | data formatting | bytes 4194304

commit v5 on v4

--- a/solution.py
+++ b/solution.py
@@ -8,7 +8,7 @@
 LX, LY, LZ, R = 16, 8, 32, 128
 ITERS = 4
 PX, PY, PZ = LX + 1 + ITERS, LY + 2, 40
-CUTS = (0, LX // 2, LX - 1)
+CUTS = (0, 9, LX - 1)
 SITES = 64 * 128 * 128
 MESH = pl.DeviceIdType.MESH
 COPIES = 88
@@ -239,10 +239,10 @@
             for i in range((ITERS - 1) * LY):
                 start = (LX * LY + i) * LZ
                 w[start:start + LZ, :] = jnp.broadcast_to(halo_t[:, i:i + 1], (LZ, R))
-        if more:
-            forward(n + 1)
         arrived(skew_z(n) + skew_y(n))
         skew_unpack(n)
+        if more:
+            forward(n + 1)
         arrived([far_copy(n, 0), far_copy(n, 1)])
         for m, k in skew(n):
             if m < n:

time: 67 us -> 66.8 us (level)
  no operation moved by 1% of the time
where the time goes in v5:
time: 66.8 us; the launch traced here: 66.6 us
  Pallas kernels  64.1 us (96%)
  local copies, waits for them, and re-layouts  1.92 us (3%)
    pallas_call x1, Pallas kernels, shards(): pl.pallas_call(kernel, out_shape=(jax.ShapeDtypeStruct((9, R), jnp.float3...  64.1 us
    unnamed x2, local copies, waits for them, and re-layouts  1.92 us

profile of v5, /device:TPU:1, one launch (start us, length us, event | category | flops | bytes accessed | tf_op | source)
XLA Modules:
  0.0 66.6 jit_solution(14504116631397218529)
XLA Ops:
  0.6 64.1 %shard_map.41 = (f32[9,128]{1,0:T(8,128)S(1)}, f32[16,8,32,128]{3,2,1,0:T(8,128)S(1)}) custom-call(f32[16,8,32,128]{3,2,1,0:T(8,128)} %v_ref.1, f32[16,8,32]{2,1,0:T(8,128)} %pot_ref.1), custom_call_target="tpu_custom_call" | custom-call | tf_op jit(solution)/shard_map/pallas_call | solution.py:316
  64.7 0.6 copy.6
  65.3 1.3 %copy.7 = f32[16,8,32,128]{3,2,1,0:T(8,128)} copy(f32[16,8,32,128]{3,2,1,0:T(8,128)S(1)} %get-tuple-element.5) | data formatting | bytes 4194304
